TPU v7x, 256 devices: a whole 4x4x8 slice. The times are simulated.
256 devices in a mesh: dp: 32 (over z, y), mp: 8 (over x, core).
Axes of the slice: x: 4, y: 4, z: 8, core: 2. Of those that a mesh axis runs over, the one named last changes fastest.
Arguments:
- embedded: bfloat16 [128, 64, 4096], P('dp', None, 'mp'), may hold values from -6 to 6
- targets: int32 [128, 64], P('dp'), may hold values from 0 to 65535
- labels: int32 [128], P('dp'), may hold values from 0 to 21
- counts: int32 [32], replicated, may hold values from 0 to 4, as said below
- destinations: int32 [128], P('dp'), may hold values from 0 to 63, as said below
- gain_in: float32 [4096], replicated, may hold values from 0.1 to 1.9
- w_query: bfloat16 [4096, 2048], P(None, 'mp'), may hold values from -40 to 40
- w_key: bfloat16 [4096, 1024], P(None, 'mp'), may hold values from -0.09375 to 0.09375
- w_value: bfloat16 [4096, 1024], P(None, 'mp'), may hold values from -0.09375 to 0.09375
- w_out: bfloat16 [2048, 4096], P('mp'), may hold values from -0.5 to 0.5
- gain_out: float32 [4096], replicated, may hold values from 0.1 to 1.9
- w_vocab: bfloat16 [4096, 65536], P('mp', 'dp'), may hold values from -40 to 40
- prev_probs: float32 [22], replicated, may hold values from 0.03 to 0.2
- log_weights: float32 [22], replicated, may hold values from -200 to 21000
Outputs:
- token_loss: float32 [4096], P(('dp', 'mp'))
- new_weights: float32 [22], replicated
- probs: float32 [22], replicated
Inputs may be any that keep to these rules, and one draw needn't show every extreme that they name: The counts sum to 64. `destinations`: each value from 0 to 63 is held by exactly one live slot; entries of slots that are not live are meaningless.
All inputs are finite; a program needn't handle non-finite values.
Results may differ from a plain program's by a relative error of at most 0.015.
The roundings to bfloat16 on the way count: a program that leaves them out, or rounds other values in their place, can miss the bound.
Values may be sent and summed in bfloat16 or wider, within the bound.
No kernel may reach another device: no remote copies, remote signals or barrier semaphores. Data moves between devices by JAX's collectives and lax.ppermute only.
A program may use at most 128 MiB of HBM per device.

v0:
```python
import math
import jax
import jax.numpy as jnp
from jax import lax
from jax.sharding import Mesh
from jax.sharding import PartitionSpec as P

HEAD_DIM = 128
DOMAINS = 22
SEQ_DEV = 2
DP = ("dp_0", "dp_1")
MP = ("mp_0", "mp_1")
DP_MP = ("dp_0", "dp_1", "mp_0", "mp_1")
norm_eps = 1e-05
rope_base = 500000.0
memory_rate = 0.9
step_rate = 0.02
explore_mass = 0.005


def side_by_side(arrays, axis, dim, along):
    widths = [math.prod(a.shape[along:]) for a in arrays]
    both = jnp.concatenate(
        [a.reshape(*a.shape[:along], w) for a, w in zip(arrays, widths)], axis=along
    )
    out = lax.all_gather(both, axis, axis=dim, tiled=True)
    parts = jnp.split(out, [sum(widths[:k]) for k in range(1, len(widths))], axis=along)
    return tuple((b.reshape(*out.shape[:along], *a.shape[along:]) for a, b in zip(arrays, parts)))


def sent_to_all(array, axis):
    length = lax.axis_size(axis)
    return lax.all_to_all(
        jnp.broadcast_to(array[None], (length, *array.shape)), axis, 0, 0, tiled=True
    )


def in_order(parts, dim):
    dims = list(parts.shape[1:])
    dims[dim] *= parts.shape[0]
    return jnp.moveaxis(parts, 0, dim).reshape(dims)


def gathered_copies(array, axis, dim):
    parts = sent_to_all(array, axis)
    return in_order(parts, dim)


def split_up(array, dim, length):
    dims = array.shape
    parts = array.reshape(*dims[:dim], length, dims[dim] // length, *dims[dim + 1 :])
    return jnp.moveaxis(parts, dim, 0)


def sum_at_owner(array, axis, dim):
    length = lax.axis_size(axis)
    parts = lax.all_to_all(split_up(array, dim, length), axis, 0, 0, tiled=True)
    return jnp.sum(parts.astype(jnp.float32), axis=0)


def gathered_by_axis(array, axes, dim):
    out = array
    for number in range(len(axes) - 1, -1, -1):
        out = lax.all_gather(out, axes[number], axis=dim, tiled=True)
    return out


def stacked_from(array, axes, sequence):
    parts = array[None]
    for k in sequence:
        parts = lax.all_gather(parts, axes[k], axis=0, tiled=True)
    held = [lax.axis_size(axes[k]) for k in reversed(sequence)]
    parts = parts.reshape(*held, *array.shape)
    turned = sorted(range(len(sequence)), key=lambda place: sequence[len(sequence) - 1 - place])
    return parts.transpose(*turned, *range(len(sequence), parts.ndim)).reshape(-1, *array.shape)


def gather_axes(array, axes, sequence, dim):
    return in_order(stacked_from(array, axes, sequence), dim)


def gathered_once(array, axis):
    leaves = jax.tree.leaves(array)
    sequence = sorted(range(len(leaves)), key=lambda k: -leaves[k].size)
    width = (1, *leaves[sequence[0]].shape)[-1]
    lines = [
        jnp.pad(leaves[k].reshape(-1), (0, -leaves[k].size % width)).reshape(-1, width)
        for k in sequence
    ]
    both, at, found = (sent_to_all(jnp.concatenate(lines), axis), 0, {})
    for k, line in zip(sequence, lines):
        piece = both[:, at : at + len(line)].reshape(len(both), -1)
        found[k] = piece[:, : leaves[k].size].reshape(-1, *leaves[k].shape)
        at += len(line)
    numbers = iter(range(len(leaves)))
    return jax.tree.map(lambda _: found[next(numbers)], array)


def combined_pairwise(pieces, combine):
    while len(jax.tree.leaves(pieces)[0]) > 1:
        pieces = jax.vmap(combine)(
            *(jax.tree.map(lambda part: part[side::2], pieces) for side in (0, 1))
        )
    return jax.tree.map(lambda part: part[0], pieces)


def merged_2(array, axis, combine):
    pieces = gathered_once(array, axis)
    return combined_pairwise(pieces, combine)


def over_copies(array, axis):
    everything = sent_to_all(array, axis)
    return jnp.sum(everything, axis=0)


def packed_total(arrays, axis):
    ends = [0]
    for a in arrays:
        ends.append(ends[-1] + a.size)
    so_far = over_copies(jnp.concatenate([a.ravel() for a in arrays]), axis)
    return tuple((so_far[b:e].reshape(a.shape) for a, b, e in zip(arrays, ends, ends[1:])))


def normalize(values, gain_vec):
    inv_rms = lax.rsqrt(jnp.mean(values * values, axis=-1, keepdims=True) + norm_eps)
    return values * inv_rms * gain_vec


def rotate_halves(tensor):
    full_width = tensor.shape[-1]
    half_width = full_width // 2
    frequency = jnp.power(
        jnp.float32(rope_base), -jnp.arange(half_width, dtype=jnp.float32) * 2.0 / full_width
    )
    angles = jnp.arange(tensor.shape[1], dtype=jnp.float32)[:, None] * frequency[None, :]
    cosine = jnp.cos(angles)[None, :, None, :]
    sine_part = jnp.sin(angles)[None, :, None, :]
    first_half = tensor[..., :half_width]
    second = tensor[..., half_width:]
    return jnp.concatenate(
        [first_half * cosine - second * sine_part, second * cosine + first_half * sine_part],
        axis=-1,
    )


def local(
    embedded,
    targets,
    labels,
    counts,
    destinations,
    gain_in,
    w_query,
    w_key,
    w_value,
    w_out,
    gain_out,
    w_vocab,
    prev_probs,
    log_weights,
):
    data_count = lax.axis_size(DP)
    data_index = lax.axis_index(DP)
    model_shard_count = lax.axis_size(MP)
    model_index = lax.axis_index(MP)
    slot_count = embedded.shape[0]
    seq_len = embedded.shape[1]
    seq_held = SEQ_DEV
    gathered_rows = (
        lax.all_gather(embedded, DP, axis=0, tiled=True),
        *side_by_side((targets, labels, destinations), DP, 0, 1),
    )
    slot_ids = jnp.arange(data_count * slot_count, dtype=jnp.int32)
    is_live = slot_ids % slot_count < counts[slot_ids // slot_count]
    wanted = data_index * seq_held + jnp.arange(seq_held, dtype=jnp.int32)
    picking_mask = (gathered_rows[3][None, :] == wanted[:, None]) & is_live[None, :]
    sequence_rows = jnp.einsum(
        "av,vyr->ayr",
        picking_mask.astype(jnp.bfloat16),
        gathered_rows[0],
        preferred_element_type=jnp.float32,
    ).astype(jnp.bfloat16)
    seq_targets = jnp.einsum("gs,sl->gl", picking_mask.astype(jnp.int32), gathered_rows[1])
    seq_labels = jnp.sum(jnp.where(picking_mask, gathered_rows[2][None, :], 0), axis=1).astype(
        jnp.int32
    )
    full_rows = gathered_copies(sequence_rows, MP, 2)
    rows_all = seq_held * seq_len
    flat_rows = full_rows.reshape(rows_all, -1).astype(jnp.float32)
    normed = normalize(flat_rows, gain_in).astype(jnp.bfloat16)
    local_heads = w_query.shape[1] // HEAD_DIM
    local_groups = w_key.shape[1] // HEAD_DIM
    query_heads = jnp.dot(normed, w_query, preferred_element_type=jnp.float32).reshape(
        seq_held, seq_len, local_heads, HEAD_DIM
    )
    key_heads = jnp.dot(normed, w_key, preferred_element_type=jnp.float32).reshape(
        seq_held, seq_len, local_groups, HEAD_DIM
    )
    value_heads = (
        jnp.dot(normed, w_value, preferred_element_type=jnp.float32)
        .astype(jnp.bfloat16)
        .reshape(seq_held, seq_len, local_groups, HEAD_DIM)
    )
    query_heads = rotate_halves(query_heads).astype(jnp.bfloat16)
    key_heads = rotate_halves(key_heads).astype(jnp.bfloat16)
    group_size = local_heads // local_groups
    key_heads = jnp.repeat(key_heads, group_size, axis=2)
    value_heads = jnp.repeat(value_heads, group_size, axis=2)
    scores = jnp.einsum(
        "sqhe,skhe->shqk", query_heads, key_heads, preferred_element_type=jnp.float32
    ) * HEAD_DIM ** (-0.5)
    causal = jnp.arange(seq_len)[:, None] >= jnp.arange(seq_len)[None, :]
    scores = jnp.where(causal[None, None], scores, -jnp.inf)
    weights = jax.nn.softmax(scores, axis=-1).astype(jnp.bfloat16)
    mixed_heads = jnp.einsum(
        "shqk,skhe->sqhe", weights, value_heads, preferred_element_type=jnp.float32
    )
    mixed_heads = mixed_heads.astype(jnp.bfloat16).reshape(rows_all, local_heads * HEAD_DIM)
    row_block_tiles = rows_all // model_shard_count
    update = sum_at_owner(
        jnp.dot(mixed_heads, w_out, preferred_element_type=jnp.float32).astype(jnp.bfloat16), MP, 0
    )
    my_start = model_index * row_block_tiles
    own_rows = lax.dynamic_slice_in_dim(flat_rows, my_start, row_block_tiles, 0)
    hidden = own_rows + update
    final_rows = normalize(hidden, gain_out).astype(jnp.bfloat16)
    own_targets = lax.dynamic_slice_in_dim(
        seq_targets.reshape(rows_all), my_start, row_block_tiles, 0
    )
    own_labels = lax.dynamic_slice_in_dim(
        jnp.repeat(seq_labels, seq_len), my_start, row_block_tiles, 0
    )
    everyone = (
        gathered_by_axis(final_rows, DP, 0),
        gathered_by_axis(own_targets, DP, 0),
        gathered_by_axis(own_labels, DP, 0),
    )
    all_rows = everyone[0]
    all_goals = everyone[1]
    all_kinds = everyone[2]
    vocab_local = w_vocab.shape[1]
    logits = jnp.dot(
        all_rows, gather_axes(w_vocab, MP, (0, 1), 0), preferred_element_type=jnp.float32
    )
    row_top = jnp.max(logits, axis=1)
    spread = jnp.sum(jnp.exp(logits - row_top[:, None]), axis=1)
    column_ids = all_goals - data_index * vocab_local
    picked = jnp.sum(
        jnp.where(
            jnp.arange(vocab_local, dtype=jnp.int32)[None, :] == column_ids[:, None], logits, 0.0
        ),
        axis=1,
    )

    def combine(earlier, later):
        larger = jnp.maximum(earlier[0], later[0])
        joined = earlier[1] * jnp.exp(earlier[0] - larger) + later[1] * jnp.exp(later[0] - larger)
        return (larger, joined, earlier[2] + later[2])

    merged = merged_2((row_top, spread, picked), DP, combine)
    top_all = merged[0]
    spread_all = merged[1]
    picked_all = merged[2]
    losses = top_all + jnp.log(spread_all) - picked_all
    own_loss = lax.dynamic_slice_in_dim(losses, data_index * row_block_tiles, row_block_tiles, 0)
    domains = jnp.arange(DOMAINS, dtype=jnp.int32)
    member = (all_kinds[:, None] == domains[None, :]).astype(jnp.float32)
    totals = packed_total((jnp.sum(member * losses[:, None], axis=0), jnp.sum(member, axis=0)), MP)
    loss_sums = totals[0]
    token_tally = totals[1]
    reward = loss_sums / jnp.maximum(token_tally, 1.0) / prev_probs
    new_weights = memory_rate * log_weights + (1.0 - memory_rate) * reward
    probs = (1.0 - DOMAINS * explore_mass) * jax.nn.softmax(step_rate * new_weights) + explore_mass
    return (own_loss, new_weights, probs)


def solution(mesh):
    torus = Mesh(mesh.devices.reshape(8, 4, 4, 2), ("dp_0", "dp_1", "mp_0", "mp_1"))
    in_specs = (
        P(DP, None, MP),
        P(DP, None),
        P(DP),
        P(),
        P(DP),
        P(),
        P(None, MP),
        P(None, MP),
        P(None, MP),
        P(MP, None),
        P(),
        P(MP, DP),
        P(),
        P(),
    )
    out_specs = (P(DP_MP), P(), P())
    return jax.shard_map(local, mesh=torus, in_specs=in_specs, out_specs=out_specs, check_vma=False)
```

profile of v0, /device:TPU:1, one launch (start us, length us, event | category | flops | bytes accessed | tf_op | source)
XLA Modules:
  0.0 396.9 jit_solution(11484693053749680303)
XLA Ops:
  7.2 0.7 all-gather.13.cloned.1.call-update
  8.0 0.7 all-gather.7.cloned.1.call-update
  8.7 90.3 %all-gather.13.cloned.1.call-done = bf16[2048,2048]{1,0:T(8,128)(2,1)} async-done(((bf16[512,2048]{1,0:T(8,128)(2,1)}), bf16[2048,2048]{1,0:T(8,128)(2,1)}) %all-gather.13.cloned.1.call-update) | async-done | bytes 8388624 | tf_op jit(solution)/shard_map/all_gather | solution.py:71
  99.1 0.6 copy-done.10
  99.7 0.1 copy.86
  99.8 0.1 copy.87
  100.0 39.4 %all-gather.1 = s32[32,4,66]{2,1,0:T(4,128)S(1)} all-gather(s32[1,4,66]{2,1,0:T(4,128)S(1)} %add_bitcast_fusion), channel_id=1, replica_groups=mesh['dp_0'=8,'dp_1'=4,'mp_0'=4,'mp_1'=2] {'dp_0','dp_1'}, dimensions={0}, use_global_device_ids=true | all-gather | bytes 34848 | tf_op jit(solution)/shard_map/all_gather | solution.py:26
  139.6 1.2 gather_fusion
  140.9 0.2 select_reduce_fusion.2
  141.1 59.0 %all-gather.7.cloned.1.call-done = bf16[128,64,512]{2,1,0:T(8,128)(2,1)} async-done(((bf16[4,64,512]{2,1,0:T(8,128)(2,1)}), bf16[128,64,512]{2,1,0:T(8,128)(2,1)}) %all-gather.7.cloned.1.call-update) | async-done | bytes 8388624 | tf_op jit(solution)/shard_map/all_gather | solution.py:171
  200.0 12.2 %fusion.7 = bf16[2,64,512]{2,0,1:T(2,128)(2,1)S(1)} fusion(bf16[128,64,512]{2,1,0:T(8,128)(2,1)} %all-gather.7.cloned.1.call-done, pred[2,128]{1,0:T(4,128)(4,1)S(1)} %get-tuple-element.22), kind=kOutput, calls=%fused_computation.19 | convolution fusion | flops 16842752 | bytes 8519936 | tf_op jit(solution)/shard_map/av,vyr->ayr/dot_general | solution.py:178
  212.3 1.1 broadcast_in_dim.39
  213.4 5.7 %all-to-all-start = ((bf16[8,2,64,512]{3,2,1,0:T(8,128)(2,1)}), bf16[8,2,64,512]{3,2,1,0:T(8,128)(2,1)S(1)}, u32[]{:S(2)}, u32[]{:S(2)}) async-start(bf16[8,2,64,512]{3,2,1,0:T(8,128)(2,1)} %broadcast_in_dim.39), calls=%async_computation | async-start | bytes 2097152 | tf_op jit(solution)/shard_map/all_to_all | solution.py:33
  219.0 4.3 %copy.104 = bf16[256,4096]{1,0:T(8,128)(2,1)} copy(bf16[256,4096]{0,1:T(8,128)(2,1)} %bitcast.86) | data formatting | bytes 4194304 | tf_op jit(solution)/shard_map/dot_general | solution.py:194
  223.4 0.1 fusion.32
  223.5 10.4 %all-to-all-done = bf16[8,2,64,512]{3,2,1,0:T(8,128)(2,1)S(1)} async-done(((bf16[8,2,64,512]{3,2,1,0:T(8,128)(2,1)}), bf16[8,2,64,512]{3,2,1,0:T(8,128)(2,1)S(1)}, u32[]{:S(2)}, u32[]{:S(2)}) %all-to-all-start) | async-done | bytes 1048608 | tf_op jit(solution)/shard_map/all_to_all | solution.py:33
  234.0 1.6 convert_bitcast_fusion.1
  235.6 1.5 copy.110
  237.1 0.3 fusion.3
  237.5 0.3 fusion.13
  237.8 1.6 copy.92
  239.4 1.6 reshape.334
  241.0 2.8 copy.91
  243.8 3.0 copy.111
  246.8 0.5 convolution_bitcast_fusion
  247.5 0.9 copy-done.3
  248.4 0.9 fusion.15
  249.3 0.1 subtract_convert_fusion
  249.4 0.3 fusion.53
  249.7 0.2 fusion.11
  249.9 2.4 convolution_convert_fusion.2
  252.3 0.2 fusion.12
  252.6 1.5 convolution_convert_fusion
  254.1 4.5 %all-to-all-start.1 = ((bf16[8,16,4096]{2,1,0:T(8,128)(2,1)}), bf16[8,16,4096]{2,1,0:T(8,128)(2,1)S(1)}, u32[]{:S(2)}, u32[]{:S(2)}) async-start(bf16[8,16,4096]{2,1,0:T(8,128)(2,1)} %bitcast.19), calls=%async_computation.1 | async-start | bytes 2097152 | tf_op jit(solution)/shard_map/all_to_all | solution.py:57
  258.7 14.9 %all-to-all-done.1 = bf16[8,16,4096]{2,1,0:T(8,128)(2,1)S(1)} async-done(((bf16[8,16,4096]{2,1,0:T(8,128)(2,1)}), bf16[8,16,4096]{2,1,0:T(8,128)(2,1)S(1)}, u32[]{:S(2)}, u32[]{:S(2)}) %all-to-all-start.1) | async-done | bytes 1048608 | tf_op jit(solution)/shard_map/all_to_all | solution.py:57
  273.6 0.1 convert_reduce_fusion
  273.8 1.1 multiply_reduce_fusion
  274.9 1.0 multiply_convert_fusion.4
  276.0 10.6 %all_gather.32 = bf16[64,4096]{1,0:T(8,128)(2,1)} all-gather(bf16[16,4096]{1,0:T(8,128)(2,1)S(1)} %multiply_convert_fusion.4), channel_id=1, replica_groups=mesh['dp_0'=8,'dp_1'=4,'mp_0'=4,'mp_1'=2] {'dp_1'}, dimensions={0}, use_global_device_ids=true | all-gather | bytes 655360 | tf_op jit(solution)/shard_map/all_gather | solution.py:64
  286.6 0.2 fusion.23
  287.0 0.6 dynamic-slice.1
  287.6 0.6 dynamic-slice.2
  289.5 0.2 dynamic-slice_dynamic-update-slice_fusion.1
  289.7 0.2 dynamic-slice_dynamic-update-slice_fusion
  289.8 5.6 %all-reduce.5 = (s32[64]{0:T(128)S(1)}, s32[64]{0:T(128)S(1)}) all-reduce(s32[64]{0:T(128)S(1)} %dynamic-slice_dynamic-update-slice_fusion.1, s32[64]{0:T(128)S(1)} %dynamic-slice_dynamic-update-slice_fusion), channel_id=1, replica_groups=mesh['dp_0'=8,'dp_1'=4,'mp_0'=4,'mp_1'=2] {'dp_1'}, use_global_device_ids=true, to_apply=%add | all-reduce | flops 128 | bytes 1024
  295.4 0.2 dynamic-update-slice.1
  295.6 0.2 dynamic-update-slice.3
  295.8 9.7 %all-reduce.4 = (s32[512]{0:T(512)S(1)}, s32[512]{0:T(512)S(1)}) all-reduce(s32[512]{0:T(512)S(1)} %dynamic-update-slice.1, s32[512]{0:T(512)S(1)} %dynamic-update-slice.3), channel_id=1, replica_groups=mesh['dp_0'=8,'dp_1'=4,'mp_0'=4,'mp_1'=2] {'dp_0'}, use_global_device_ids=true, to_apply=%add.1 | all-reduce | flops 1024 | bytes 8192
  305.6 14.2 %copy.97 = bf16[4,2,512,2048]{3,2,1,0:T(8,128)(2,1)} copy(bf16[4,2,512,2048]{3,2,0,1:T(8,128)(2,1)} %bitcast.77) | data formatting | bytes 33554432 | tf_op jit(solution)/shard_map/transpose | solution.py:75
  319.7 20.8 %all-gather.9.cloned.1.call-done = bf16[512,4096]{1,0:T(8,128)(2,1)} async-done(((bf16[64,4096]{1,0:T(8,128)(2,1)}), bf16[512,4096]{1,0:T(8,128)(2,1)}) %all-gather.9.cloned.1.call-update) | async-done | bytes 4194320 | tf_op jit(solution)/shard_map/all_gather | solution.py:64
  340.6 13.1 %fusion.58 = (f32[512]{0:T(512)S(1)}, f32[512,2048]{1,0:T(8,128)S(1)}) fusion(bf16[512,4096]{1,0:T(8,128)(2,1)} %all-gather.9.cloned.1.call-done, bf16[4096,2048]{1,0:T(8,128)(2,1)} %bitcast.78), kind=kOutput, calls=%fused_computation.113 | convolution fusion | flops 8590983168 | bytes 25167872 | tf_op jit(solution)/shard_map/dot_general | solution.py:243
  353.7 1.1 exponential_reduce_fusion
  354.9 0.7 broadcast_in_dim.44
  355.6 7.0 %all-to-all-start.2 = ((f32[32,3,512]{2,1,0:T(4,128)}), f32[32,3,512]{2,1,0:T(4,128)S(1)}, u32[]{:S(2)}, u32[]{:S(2)}) async-start(f32[32,3,512]{2,1,0:T(4,128)} %broadcast_in_dim.44), calls=%async_computation.2 | async-start | bytes 524288 | tf_op jit(solution)/shard_map/all_to_all | solution.py:33
  362.6 11.2 %all-to-all-done.2 = f32[32,3,512]{2,1,0:T(4,128)S(1)} async-done(((f32[32,3,512]{2,1,0:T(4,128)}), f32[32,3,512]{2,1,0:T(4,128)S(1)}, u32[]{:S(2)}, u32[]{:S(2)}) %all-to-all-start.2) | async-done | bytes 196640 | tf_op jit(solution)/shard_map/all_to_all | solution.py:33
  373.8 0.1 fusion.51
  374.7 0.1 select_reduce_fusion.1
  374.9 0.6 broadcast_in_dim.50
  375.5 6.6 %all-to-all-start.3 = ((f32[8,1,44]{2,1,0:T(1,128)}), f32[8,1,44]{2,1,0:T(1,128)S(1)}, u32[]{:S(2)}, u32[]{:S(2)}) async-start(f32[8,1,44]{2,1,0:T(1,128)} %broadcast_in_dim.50), calls=%async_computation.3 | async-start | bytes 8192 | tf_op jit(solution)/shard_map/all_to_all | solution.py:33
  382.1 0.6 dynamic-slice_bitcast_fusion
  382.6 4.0 %all-to-all-done.3 = f32[8,1,44]{2,1,0:T(1,128)S(1)} async-done(((f32[8,1,44]{2,1,0:T(1,128)}), f32[8,1,44]{2,1,0:T(1,128)S(1)}, u32[]{:S(2)}, u32[]{:S(2)}) %all-to-all-start.3) | async-done | bytes 1440 | tf_op jit(solution)/shard_map/all_to_all | solution.py:33
  386.7 0.7 multiply_reduce_fusion.1
  387.4 1.2 fusion.50
  388.6 1.7 multiply_add_fusion.4
  (101 shorter events, 2.0 us)
Async XLA Ops:
  7.2 245.4 %copy-start = (bf16[256,4096]{1,0:T(8,128)(2,1)S(1)}, bf16[256,4096]{1,0:T(8,128)(2,1)}, u32[]{:S(2)}) copy-start(bf16[256,4096]{1,0:T(8,128)(2,1)} %param.23) | copy-start | bytes 6291460
  7.2 91.9 %all-gather.13.cloned.1.call-start = ((), (), s32[]{:S(2)}) async-start(), calls=%async_computation.7 | async-start | bytes 10485760 | tf_op jit(solution)/shard_map/all_gather | solution.py:71
  7.9 192.1 %all-gather.7.cloned.1.call-start = ((), (), s32[]{:S(2)}) async-start(), calls=%async_computation.4 | async-start | bytes 8650752 | tf_op jit(solution)/shard_map/all_gather | solution.py:171
  8.7 296.9 %all-gather.11.cloned.1.call-start = ((), (), s32[]{:S(2)}) async-start(), calls=%async_computation.6 | async-start | bytes 25165824 | tf_op jit(solution)/shard_map/all_gather | solution.py:71
  99.1 0.7 copy-start.10
  99.1 0.7 copy-start.11
  99.1 0.8 copy-start.8
  99.1 40.6 %copy-start.2 = (s32[32]{0:T(128)S(1)}, s32[32]{0:T(128)}, u32[]{:S(2)}) copy-start(s32[32]{0:T(128)} %param.17) | copy-start | bytes 388
  212.3 6.8 %copy-start.6 = (f32[4096]{0:T(1024)S(1)}, f32[4096]{0:T(1024)}, u32[]{:S(2)}) copy-start(f32[4096]{0:T(1024)} %param.19) | copy-start | bytes 49156
  213.4 20.6 %all-to-all-start = ((bf16[8,2,64,512]{3,2,1,0:T(8,128)(2,1)}), bf16[8,2,64,512]{3,2,1,0:T(8,128)(2,1)S(1)}, u32[]{:S(2)}, u32[]{:S(2)}) async-start(bf16[8,2,64,512]{3,2,1,0:T(8,128)(2,1)} %broadcast_in_dim.39), calls=%async_computation | async-start | bytes 2097152 | tf_op jit(solution)/shard_map/all_to_all | solution.py:33
  243.8 3.0 copy-start.4
  243.8 3.0 copy-start.5
  246.8 1.6 copy-start.3
  254.1 20.8 %copy-start.7 = (f32[4096]{0:T(1024)S(1)}, f32[4096]{0:T(1024)}, u32[]{:S(2)}) copy-start(f32[4096]{0:T(1024)} %param.24) | copy-start | bytes 49156
  254.1 19.5 %all-to-all-start.1 = ((bf16[8,16,4096]{2,1,0:T(8,128)(2,1)}), bf16[8,16,4096]{2,1,0:T(8,128)(2,1)S(1)}, u32[]{:S(2)}, u32[]{:S(2)}) async-start(bf16[8,16,4096]{2,1,0:T(8,128)(2,1)} %bitcast.19), calls=%async_computation.1 | async-start | bytes 2097152 | tf_op jit(solution)/shard_map/all_to_all | solution.py:57
  258.6 28.4 %copy-start.15 = (u32[256]{0:T(256)S(1)}, u32[256]{0:T(256)}, u32[]{:S(2)}) copy-start(u32[256]{0:T(256)} %constant.102) | copy-start | bytes 3076
  258.6 29.0 %copy-start.14 = (u32[256]{0:T(256)S(1)}, u32[256]{0:T(256)}, u32[]{:S(2)}) copy-start(u32[256]{0:T(256)} %constant.107) | copy-start | bytes 3076
  258.7 81.9 %all-gather.9.cloned.1.call-start = ((), (), s32[]{:S(2)}) async-start(), calls=%async_computation.5 | async-start | bytes 4718592 | tf_op jit(solution)/shard_map/all_gather | solution.py:64
  353.7 36.6 %copy-start.1 = (bf16[256,4096]{1,0:T(8,128)(2,1)S(1)}, bf16[256,4096]{1,0:T(8,128)(2,1)}, u32[]{:S(2)}) copy-start(bf16[256,4096]{1,0:T(8,128)(2,1)} %param.23) | copy-start | bytes 6291460
  354.9 31.8 %copy-start.12 = (f32[22]{0:T(128)S(1)}, f32[22]{0:T(128)}, u32[]{:S(2)}) copy-start(f32[22]{0:T(128)} %param.26) | copy-start | bytes 268
  354.9 31.8 %copy-start.13 = (f32[22]{0:T(128)S(1)}, f32[22]{0:T(128)}, u32[]{:S(2)}) copy-start(f32[22]{0:T(128)} %param.27) | copy-start | bytes 268
  355.6 18.2 %all-to-all-start.2 = ((f32[32,3,512]{2,1,0:T(4,128)}), f32[32,3,512]{2,1,0:T(4,128)S(1)}, u32[]{:S(2)}, u32[]{:S(2)}) async-start(f32[32,3,512]{2,1,0:T(4,128)} %broadcast_in_dim.44), calls=%async_computation.2 | async-start | bytes 524288 | tf_op jit(solution)/shard_map/all_to_all | solution.py:33
  375.5 11.2 %all-to-all-start.3 = ((f32[8,1,44]{2,1,0:T(1,128)}), f32[8,1,44]{2,1,0:T(1,128)S(1)}, u32[]{:S(2)}, u32[]{:S(2)}) async-start(f32[8,1,44]{2,1,0:T(1,128)} %broadcast_in_dim.50), calls=%async_computation.3 | async-start | bytes 8192 | tf_op jit(solution)/shard_map/all_to_all | solution.py:33
  387.4 3.0 copy-start.9
Sparse Core Ops, SparseCore 0:
  9.8 89.2 all-gather.12
  101.6 98.3 all-gather.6
  201.8 33.9 all-gather.10
  286.7 53.7 all-gather.8
where the time goes:
time: 398 us; the launch traced here: 397 us
  waiting for transfers between devices  212 us (53%)
  blocking collectives  65.3 us (16%)
  local copies, waits for them, and re-layouts  38.1 us (10%)
  matrix products  31.5 us (8%)
  starting transfers between devices  23.9 us (6%)
  between operations  15.4 us (4%)
  other arithmetic  10.5 us (3%)
    all_gather x2, waiting for transfers between devices, stacked_from(): parts = lax.all_gather(parts, axes[k], axis=0, tiled=True)  90.3 us
    all_gather x1, waiting for transfers between devices, local(): lax.all_gather(embedded, DP, axis=0, tiled=True)  59 us
    all_gather x1, blocking collectives, side_by_side(): out = lax.all_gather(both, axis, axis=dim, tiled=True)  39.4 us
    all_to_all x3, waiting for transfers between devices, sent_to_all(): lax.all_to_all(jnp.broadcast_to(array[None], (length, *array.shape)), axi...  25.7 us
    all_gather x1, waiting for transfers between devices, gathered_by_axis(): out = lax.all_gather(out, axes[number], axis=dim, tiled=True)  20.8 us
    all_to_all x3, starting transfers between devices, sent_to_all(): lax.all_to_all(jnp.broadcast_to(array[None], (length, *array.shape)), axi...  19.2 us
    unnamed x2, blocking collectives  15.3 us
    all_to_all x1, waiting for transfers between devices, sum_at_owner(): parts = lax.all_to_all(split_up(array, dim, length), axis, 0, 0, tiled=True)  14.9 us
  transfers between devices with their start and end apart: 8, of which 7 were waited for; matrix products, arithmetic and copies ran while one was open for 15% of the time, Pallas kernels for 0%

commit v1 on v0

--- a/solution.py
+++ b/solution.py
@@ -168,7 +168,12 @@
     seq_len = embedded.shape[1]
     seq_held = SEQ_DEV
     gathered_rows = (
-        lax.all_gather(embedded, DP, axis=0, tiled=True),
+        jnp.concatenate(
+            jax.lax.all_to_all(
+                jnp.stack([embedded for _ in range(jax.lax.axis_size(DP))]), DP, 0, 0
+            ),
+            0,
+        ),
         *side_by_side((targets, labels, destinations), DP, 0, 1),
     )
     slot_ids = jnp.arange(data_count * slot_count, dtype=jnp.int32)

time: 398 us -> 475 us (1.19)
  blocking collectives: 65.3 us -> 178 us
  waiting for transfers between devices: 212 us -> 134 us
  local copies, waits for them, and re-layouts: 38.1 us -> 64.6 us
  starting transfers between devices: 23.9 us -> 47.2 us
  matrix products: 31.5 us -> 25.1 us
    all_gather x1, blocking collectives: 39.4 us -> 153 us  [side_by_side(): out = lax.all_gather(both, axis, axis=dim, tiled=True)]
    all_gather x1 -> x0, waiting for transfers between devices: 59 us -> none  [local(): lax.all_gather(embedded, DP, axis=0, tiled=True)]
    all_gather x2, waiting for transfers between devices: 90.3 us -> 71.4 us  [stacked_from(): parts = lax.all_gather(parts, axes[k], axis=0, tiled=True)]
    reshape x0 -> x1, local copies, waits for them, and re-layouts: none -> 12.5 us  [local(): jnp.concatenate(jax.lax.all_to_all(jnp.stack([embedded for _ in range(jax...]
    all_to_all x0 -> x1, starting transfers between devices: none -> 12.2 us  [local(): jax.lax.all_to_all(jnp.stack([embedded for _ in range(jax.lax.axis_size(D...]
    all_to_all x3, starting transfers between devices: 19.2 us -> 30.4 us  [sent_to_all(): lax.all_to_all(jnp.broadcast_to(array[None], (length, *array.shape)), axi...]
    all_to_all x0 -> x1, local copies, waits for them, and re-layouts: none -> 8.11 us  [local(): jax.lax.all_to_all(jnp.stack([embedded for _ in range(jax.lax.axis_size(D...]
    dot_general x1, matrix products: 12.2 us -> 4.57 us  [local(): jnp.einsum('av,vyr->ayr', picking_mask.astype(jnp.bfloat16), gathered_row...]
  transfers between devices with their start and end apart: 8 -> 8, of which waited for: 7 -> 6; matrix products, arithmetic and copies ran while one was open for 15% -> 16% of each run, Pallas kernels for 0% -> 0%
where the time goes in v1:
time: 475 us; the launch traced here: 474 us
  blocking collectives  178 us (37%)
  waiting for transfers between devices  134 us (28%)
  local copies, waits for them, and re-layouts  64.6 us (14%)
  starting transfers between devices  47.2 us (10%)
  matrix products  25.1 us (5%)
  between operations  15.5 us (3%)
  other arithmetic  9.34 us (2%)
    all_gather x1, blocking collectives, side_by_side(): out = lax.all_gather(both, axis, axis=dim, tiled=True)  153 us
    all_gather x2, waiting for transfers between devices, stacked_from(): parts = lax.all_gather(parts, axes[k], axis=0, tiled=True)  71.4 us
    all_to_all x3, starting transfers between devices, sent_to_all(): lax.all_to_all(jnp.broadcast_to(array[None], (length, *array.shape)), axi...  30.4 us
    all_to_all x3, waiting for transfers between devices, sent_to_all(): lax.all_to_all(jnp.broadcast_to(array[None], (length, *array.shape)), axi...  25.9 us
    all_gather x1, waiting for transfers between devices, gathered_by_axis(): out = lax.all_gather(out, axes[number], axis=dim, tiled=True)  21.3 us
    all_to_all x1, waiting for transfers between devices, sum_at_owner(): parts = lax.all_to_all(split_up(array, dim, length), axis, 0, 0, tiled=True)  14.9 us
    transpose x1, local copies, waits for them, and re-layouts, stacked_from(): parts.transpose(*turned, *range(len(sequence), parts.ndim))  14.2 us
    unnamed x2, blocking collectives  14.2 us
  transfers between devices with their start and end apart: 8, of which 6 were waited for; matrix products, arithmetic and copies ran while one was open for 16% of the time, Pallas kernels for 0%

profile of v1, /device:TPU:1, one launch (start us, length us, event | category | flops | bytes accessed | tf_op | source)
XLA Modules:
  0.0 473.9 jit_solution(17950624504261966114)
XLA Ops:
  7.2 0.7 all-gather.10.cloned.1.call-update
  7.9 0.4 copy-done.7
  8.3 0.2 copy.92
  8.5 7.0 %stack.2 = bf16[32,4,64,512]{3,1,2,0:T(4,128)(2,1)} broadcast(bf16[4,64,512]{2,0,1:T(4,128)(2,1)S(1)} %copy.92), dimensions={1,2,3} | broadcast | bytes 8650752 | tf_op jit(solution)/shard_map/stack | solution.py:173
  15.5 12.2 %all-to-all-start = ((bf16[32,4,64,512]{3,1,2,0:T(4,128)(2,1)}), bf16[32,4,64,512]{3,1,2,0:T(4,128)(2,1)}, u32[]{:S(2)}, u32[]{:S(2)}) async-start(bf16[32,4,64,512]{3,1,2,0:T(4,128)(2,1)} %stack.2), calls=%async_computation | async-start | bytes 16777216 | tf_op jit(solution)/shard_map/all_to_all | solution.py:172
  27.7 71.4 %all-gather.10.cloned.1.call-done = bf16[2048,2048]{1,0:T(8,128)(2,1)} async-done(((bf16[512,2048]{1,0:T(8,128)(2,1)}), bf16[2048,2048]{1,0:T(8,128)(2,1)}) %all-gather.10.cloned.1.call-update) | async-done | bytes 8388624 | tf_op jit(solution)/shard_map/all_gather | solution.py:71
  99.1 0.6 copy-done.12
  100.0 153.2 %all-gather.1 = s32[32,4,66]{2,1,0:T(4,128)S(1)} all-gather(s32[1,4,66]{2,1,0:T(4,128)S(1)} %add_bitcast_fusion), channel_id=1, replica_groups=mesh['dp_0'=8,'dp_1'=4,'mp_0'=4,'mp_1'=2] {'dp_0','dp_1'}, dimensions={0}, use_global_device_ids=true | all-gather | bytes 34848 | tf_op jit(solution)/shard_map/all_gather | solution.py:26
  253.5 1.2 gather_fusion
  254.8 0.2 select_reduce_fusion.2
  254.9 8.1 %copy.93 = bf16[32,4,64,512]{3,1,0,2:T(4,128)(2,1)} copy(bf16[32,4,64,512]{3,1,2,0:T(4,128)(2,1)} %all-to-all-done) | data formatting | bytes 16777216 | tf_op jit(solution)/shard_map/all_to_all | solution.py:172
  263.1 12.5 %reshape.291 = bf16[128,64,512]{2,0,1:T(8,128)(2,1)} reshape(bf16[32,4,64,512]{3,1,0,2:T(4,128)(2,1)} %copy.93) | data formatting | bytes 16777216 | tf_op jit(solution)/shard_map/reshape | solution.py:171
  275.6 4.6 convolution_convert_fusion.1
  280.2 1.1 broadcast_in_dim.39
  281.3 16.8 %all-to-all-start.1 = ((bf16[8,2,64,512]{3,2,1,0:T(8,128)(2,1)}), bf16[8,2,64,512]{3,2,1,0:T(8,128)(2,1)S(1)}, u32[]{:S(2)}, u32[]{:S(2)}) async-start(bf16[8,2,64,512]{3,2,1,0:T(8,128)(2,1)} %broadcast_in_dim.39), calls=%async_computation.1 | async-start | bytes 2097152 | tf_op jit(solution)/shard_map/all_to_all | solution.py:33
  298.1 4.1 copy.108
  302.3 0.1 fusion.27
  302.4 10.7 %all-to-all-done.1 = bf16[8,2,64,512]{3,2,1,0:T(8,128)(2,1)S(1)} async-done(((bf16[8,2,64,512]{3,2,1,0:T(8,128)(2,1)}), bf16[8,2,64,512]{3,2,1,0:T(8,128)(2,1)S(1)}, u32[]{:S(2)}, u32[]{:S(2)}) %all-to-all-start.1) | async-done | bytes 1048608 | tf_op jit(solution)/shard_map/all_to_all | solution.py:33
  313.1 0.3 fusion.1
  313.5 0.3 fusion.8
  313.8 1.6 copy.96
  315.4 2.4 reshape.340
  317.8 0.6 convert_bitcast_fusion.1
  318.4 1.2 copy.95
  319.6 3.0 copy.115
  322.6 0.2 copy.114
  322.8 1.0 copy-done.5
  323.8 0.5 convolution_bitcast_fusion
  324.6 0.3 copy-done.4
  324.8 0.8 fusion.10
  325.8 0.3 fusion.48
  326.1 0.9 fusion.6
  327.0 2.1 convolution_convert_fusion.3
  329.0 1.2 fusion.7
  330.4 1.4 convolution_convert_fusion
  331.8 4.5 all-to-all-start.2
  336.4 14.9 %all-to-all-done.2 = bf16[8,16,4096]{2,1,0:T(8,128)(2,1)S(1)} async-done(((bf16[8,16,4096]{2,1,0:T(8,128)(2,1)}), bf16[8,16,4096]{2,1,0:T(8,128)(2,1)S(1)}, u32[]{:S(2)}, u32[]{:S(2)}) %all-to-all-start.2) | async-done | bytes 1048608 | tf_op jit(solution)/shard_map/all_to_all | solution.py:57
  351.3 0.1 convert_reduce_fusion
  351.5 1.1 multiply_reduce_fusion
  352.6 1.0 multiply_convert_fusion.4
  353.6 10.6 %all_gather.28 = bf16[64,4096]{1,0:T(8,128)(2,1)} all-gather(bf16[16,4096]{1,0:T(8,128)(2,1)S(1)} %multiply_convert_fusion.4), channel_id=1, replica_groups=mesh['dp_0'=8,'dp_1'=4,'mp_0'=4,'mp_1'=2] {'dp_1'}, dimensions={0}, use_global_device_ids=true | all-gather | bytes 655360 | tf_op jit(solution)/shard_map/all_gather | solution.py:64
  364.3 0.6 dynamic-slice.2
  364.9 0.6 dynamic-slice.1
  365.5 0.2 fusion.18
  367.2 0.2 dynamic-slice_dynamic-update-slice_fusion.1
  367.4 0.2 dynamic-slice_dynamic-update-slice_fusion
  367.5 5.3 %all-reduce.5 = (s32[64]{0:T(128)S(1)}, s32[64]{0:T(128)S(1)}) all-reduce(s32[64]{0:T(128)S(1)} %dynamic-slice_dynamic-update-slice_fusion.1, s32[64]{0:T(128)S(1)} %dynamic-slice_dynamic-update-slice_fusion), channel_id=1, replica_groups=mesh['dp_0'=8,'dp_1'=4,'mp_0'=4,'mp_1'=2] {'dp_1'}, use_global_device_ids=true, to_apply=%add | all-reduce | flops 128 | bytes 1024
  372.8 0.2 dynamic-update-slice.1
  373.0 0.2 dynamic-update-slice.3
  373.2 8.9 %all-reduce.4 = (s32[512]{0:T(512)S(1)}, s32[512]{0:T(512)S(1)}) all-reduce(s32[512]{0:T(512)S(1)} %dynamic-update-slice.1, s32[512]{0:T(512)S(1)} %dynamic-update-slice.3), channel_id=1, replica_groups=mesh['dp_0'=8,'dp_1'=4,'mp_0'=4,'mp_1'=2] {'dp_0'}, use_global_device_ids=true, to_apply=%add.1 | all-reduce | flops 1024 | bytes 8192
  382.1 14.2 %copy.101 = bf16[4,2,512,2048]{3,2,1,0:T(8,128)(2,1)} copy(bf16[4,2,512,2048]{3,2,0,1:T(8,128)(2,1)} %bitcast.80) | data formatting | bytes 33554432 | tf_op jit(solution)/shard_map/transpose | solution.py:75
  396.3 21.3 %all-gather.6.cloned.1.call-done = bf16[512,4096]{1,0:T(8,128)(2,1)} async-done(((bf16[64,4096]{1,0:T(8,128)(2,1)}), bf16[512,4096]{1,0:T(8,128)(2,1)}) %all-gather.6.cloned.1.call-update) | async-done | bytes 4194320 | tf_op jit(solution)/shard_map/all_gather | solution.py:64
  417.6 13.1 %fusion.53 = (f32[512]{0:T(512)S(1)}, f32[512,2048]{1,0:T(8,128)S(1)}) fusion(bf16[512,4096]{1,0:T(8,128)(2,1)} %all-gather.6.cloned.1.call-done, bf16[4096,2048]{1,0:T(8,128)(2,1)} %bitcast.81), kind=kOutput, calls=%fused_computation.111 | convolution fusion | flops 8590983168 | bytes 25167872 | tf_op jit(solution)/shard_map/dot_general | solution.py:248
  430.8 1.1 exponential_reduce_fusion
  431.9 0.7 broadcast_in_dim.44
  432.7 7.0 %all-to-all-start.3 = ((f32[32,3,512]{2,1,0:T(4,128)}), f32[32,3,512]{2,1,0:T(4,128)S(1)}, u32[]{:S(2)}, u32[]{:S(2)}) async-start(f32[32,3,512]{2,1,0:T(4,128)} %broadcast_in_dim.44), calls=%async_computation.3 | async-start | bytes 524288 | tf_op jit(solution)/shard_map/all_to_all | solution.py:33
  439.6 11.2 %all-to-all-done.3 = f32[32,3,512]{2,1,0:T(4,128)S(1)} async-done(((f32[32,3,512]{2,1,0:T(4,128)}), f32[32,3,512]{2,1,0:T(4,128)S(1)}, u32[]{:S(2)}, u32[]{:S(2)}) %all-to-all-start.3) | async-done | bytes 196640 | tf_op jit(solution)/shard_map/all_to_all | solution.py:33
  451.9 0.6 broadcast_in_dim.50
  452.5 6.6 %all-to-all-start.4 = ((f32[8,1,44]{2,1,0:T(1,128)}), f32[8,1,44]{2,1,0:T(1,128)S(1)}, u32[]{:S(2)}, u32[]{:S(2)}) async-start(f32[8,1,44]{2,1,0:T(1,128)} %broadcast_in_dim.50), calls=%async_computation.4 | async-start | bytes 8192 | tf_op jit(solution)/shard_map/all_to_all | solution.py:33
  459.1 0.6 dynamic-slice_bitcast_fusion
  459.7 4.0 all-to-all-done.4
  463.8 0.7 multiply_reduce_fusion.1
  464.4 1.2 fusion.45
  465.7 1.7 multiply_add_fusion.4
  (108 shorter events, 2.6 us)
Async XLA Ops:
  7.2 323.2 %copy-start = (bf16[256,4096]{1,0:T(8,128)(2,1)S(1)}, bf16[256,4096]{1,0:T(8,128)(2,1)}, u32[]{:S(2)}) copy-start(bf16[256,4096]{1,0:T(8,128)(2,1)} %param.23) | copy-start | bytes 6291460
  7.2 1.1 copy-start.7
  7.2 91.9 %all-gather.10.cloned.1.call-start = ((), (), s32[]{:S(2)}) async-start(), calls=%async_computation.7 | async-start | bytes 10485760 | tf_op jit(solution)/shard_map/all_gather | solution.py:71
  15.5 239.5 %all-to-all-start = ((bf16[32,4,64,512]{3,1,2,0:T(4,128)(2,1)}), bf16[32,4,64,512]{3,1,2,0:T(4,128)(2,1)}, u32[]{:S(2)}, u32[]{:S(2)}) async-start(bf16[32,4,64,512]{3,1,2,0:T(4,128)(2,1)} %stack.2), calls=%async_computation | async-start | bytes 16777216 | tf_op jit(solution)/shard_map/all_to_all | solution.py:172
  27.6 354.5 %all-gather.8.cloned.1.call-start = ((), (), s32[]{:S(2)}) async-start(), calls=%async_computation.6 | async-start | bytes 25165824 | tf_op jit(solution)/shard_map/all_gather | solution.py:71
  99.1 0.7 copy-start.12
  99.1 0.7 copy-start.13
  99.1 0.8 copy-start.10
  99.1 154.4 %copy-start.2 = (s32[32]{0:T(128)S(1)}, s32[32]{0:T(128)}, u32[]{:S(2)}) copy-start(s32[32]{0:T(128)} %param.17) | copy-start | bytes 388
  280.1 18.0 %copy-start.8 = (f32[4096]{0:T(1024)S(1)}, f32[4096]{0:T(1024)}, u32[]{:S(2)}) copy-start(f32[4096]{0:T(1024)} %param.19) | copy-start | bytes 49156
  281.3 31.8 %all-to-all-start.1 = ((bf16[8,2,64,512]{3,2,1,0:T(8,128)(2,1)}), bf16[8,2,64,512]{3,2,1,0:T(8,128)(2,1)S(1)}, u32[]{:S(2)}, u32[]{:S(2)}) async-start(bf16[8,2,64,512]{3,2,1,0:T(8,128)(2,1)} %broadcast_in_dim.39), calls=%async_computation.1 | async-start | bytes 2097152 | tf_op jit(solution)/shard_map/all_to_all | solution.py:33
  322.6 1.2 copy-start.5
  322.8 1.7 copy-start.3
  322.8 2.0 copy-start.4
  324.8 2.1 copy-start.6
  331.8 20.8 %copy-start.9 = (f32[4096]{0:T(1024)S(1)}, f32[4096]{0:T(1024)}, u32[]{:S(2)}) copy-start(f32[4096]{0:T(1024)} %param.24) | copy-start | bytes 49156
  331.8 19.5 %all-to-all-start.2 = ((bf16[8,16,4096]{2,1,0:T(8,128)(2,1)}), bf16[8,16,4096]{2,1,0:T(8,128)(2,1)S(1)}, u32[]{:S(2)}, u32[]{:S(2)}) async-start(bf16[8,16,4096]{2,1,0:T(8,128)(2,1)} %bitcast.19), calls=%async_computation.2 | async-start | bytes 2097152 | tf_op jit(solution)/shard_map/all_to_all | solution.py:57
  336.3 28.0 %copy-start.17 = (u32[256]{0:T(256)S(1)}, u32[256]{0:T(256)}, u32[]{:S(2)}) copy-start(u32[256]{0:T(256)} %constant.107) | copy-start | bytes 3076
  336.3 28.6 %copy-start.16 = (u32[256]{0:T(256)S(1)}, u32[256]{0:T(256)}, u32[]{:S(2)}) copy-start(u32[256]{0:T(256)} %constant.102) | copy-start | bytes 3076
  336.3 81.3 %all-gather.6.cloned.1.call-start = ((), (), s32[]{:S(2)}) async-start(), calls=%async_computation.5 | async-start | bytes 4718592 | tf_op jit(solution)/shard_map/all_gather | solution.py:64
  430.8 36.6 %copy-start.1 = (bf16[256,4096]{1,0:T(8,128)(2,1)S(1)}, bf16[256,4096]{1,0:T(8,128)(2,1)}, u32[]{:S(2)}) copy-start(bf16[256,4096]{1,0:T(8,128)(2,1)} %param.23) | copy-start | bytes 6291460
  431.9 31.9 %copy-start.14 = (f32[22]{0:T(128)S(1)}, f32[22]{0:T(128)}, u32[]{:S(2)}) copy-start(f32[22]{0:T(128)} %param.26) | copy-start | bytes 268
  431.9 31.9 %copy-start.15 = (f32[22]{0:T(128)S(1)}, f32[22]{0:T(128)}, u32[]{:S(2)}) copy-start(f32[22]{0:T(128)} %param.27) | copy-start | bytes 268
  432.7 18.2 %all-to-all-start.3 = ((f32[32,3,512]{2,1,0:T(4,128)}), f32[32,3,512]{2,1,0:T(4,128)S(1)}, u32[]{:S(2)}, u32[]{:S(2)}) async-start(f32[32,3,512]{2,1,0:T(4,128)} %broadcast_in_dim.44), calls=%async_computation.3 | async-start | bytes 524288 | tf_op jit(solution)/shard_map/all_to_all | solution.py:33
  452.5 11.2 %all-to-all-start.4 = ((f32[8,1,44]{2,1,0:T(1,128)}), f32[8,1,44]{2,1,0:T(1,128)S(1)}, u32[]{:S(2)}, u32[]{:S(2)}) async-start(f32[8,1,44]{2,1,0:T(1,128)} %broadcast_in_dim.50), calls=%async_computation.4 | async-start | bytes 8192 | tf_op jit(solution)/shard_map/all_to_all | solution.py:33
  464.4 2.9 copy-start.11
Sparse Core Ops, SparseCore 0:
  9.8 89.2 all-gather.9
  100.9 37.2 all-gather.7
  364.4 53.1 all-gather.5
